TPU v7x, 256 devices: a 2x2x32 block of a 4x8x32 slice. The times are simulated.
256 devices in a mesh: groups: 4 (over y, x), expert: 64 (over z, core).
Axes of the slice: x: 2, y: 2, z: 32, core: 2. Of those that a mesh axis runs over, the one named last changes fastest.
The devices are a block of a 4x8x32 slice.
Arguments:
- tokens: bfloat16 [4096, 6144], P(('groups', 'expert')), parts along dimension 0, may hold values from -6 to 6
- route_ids: int32 [4096, 2], P(('groups', 'expert')), parts along dimension 0, may hold values from 0 to 7, all different within a row; in each aligned block of 16 rows (0 to 15, 16 to 31, ...) at most 6 rows name the same one
- route_logits: float32 [4096, 2], P(('groups', 'expert')), parts along dimension 0, may hold values from -6 to 6
- old_place: int32 [64], replicated, may hold values from 0 to 63, each once
- new_place: int32 [64], replicated, may hold values from 0 to 63, each once
- held_gate: bfloat16 [256, 6144, 128], P(('groups', 'expert')), parts along dimension 0, may hold values from -0.078125 to 0.078125
- held_up: bfloat16 [256, 6144, 128], P(('groups', 'expert')), parts along dimension 0, may hold values from -0.078125 to 0.078125
- held_down: bfloat16 [256, 6144, 128], P(('groups', 'expert')), parts along dimension 0, may hold values from -0.1875 to 0.1875
Outputs:
- moe_output: bfloat16 [4096, 6144], P(('groups', 'expert')), parts along dimension 0
- moved_gate: bfloat16 [256, 6144, 128], P(('groups', 'expert')), parts along dimension 0
- moved_up: bfloat16 [256, 6144, 128], P(('groups', 'expert')), parts along dimension 0
- moved_down: bfloat16 [256, 6144, 128], P(('groups', 'expert')), parts along dimension 0
There are 4 independent parts, one for each index of `groups`. A program takes and returns all parts, laid end to end along the dimension named above; an argument that names none is the same for every part. Nothing has to cross between parts.
Inputs may be any that keep to these rules, and one draw needn't show every extreme that they name: `route_ids`: within the rows of one device (aligned blocks of 16 rows) no expert is named by more than 6 rows, a bound that some block reaches; the two ids of a row differ. `old_place`: each device appears once. `new_place`: each device appears once.
All inputs are finite; a program needn't handle non-finite values.
Results may differ from a plain program's by a relative error of at most 0.0058.
Values may be sent and summed in bfloat16 or wider, within the bound.
No kernel may reach another device: no remote copies, remote signals or barrier semaphores. Data moves between devices by JAX's collectives and lax.ppermute only.
A program may use at most 128 MiB of HBM per device.

v0:
```python
import jax
import jax.numpy as jnp
from jax import lax
from jax.sharding import PartitionSpec as P

EXPERTS = 8
CAP = 6


def in_one_piece(arrays, axis, split_dim, concat_dim, along):
    both = jnp.concatenate(arrays, axis=along)
    out, at, gathered = (
        lax.all_to_all(both, axis, split_axis=split_dim, concat_axis=concat_dim, tiled=True),
        0,
        [],
    )
    for a in arrays:
        gathered.append(lax.slice_in_dim(out, at, at + a.shape[along], axis=along))
        at += a.shape[along]
    return tuple(gathered)


def inverse_of(placement, device_ids):
    return jnp.sum(
        jnp.where(placement[:, None] == device_ids[None, :], device_ids[:, None], 0), axis=0
    )


def per_device(
    tokens, route_ids, route_logits, old_place, new_place, held_gate, held_up, held_down
):
    devices = lax.axis_size("expert")
    width = tokens.shape[1]
    tok_rows = tokens.shape[0]
    device_ids = jnp.arange(devices, dtype=jnp.int32)
    slot_new_at = inverse_of(new_place, device_ids)
    slot_old_at = inverse_of(old_place, device_ids)
    source_of = jnp.take(old_place, slot_new_at)
    pieces = in_one_piece((held_gate, held_up, held_down), "expert", 1, 0, 2)
    reordered = (
        jnp.take(pieces[0], source_of, axis=0),
        jnp.take(pieces[1], source_of, axis=0),
        jnp.take(pieces[2], source_of, axis=0),
    )
    migrated = in_one_piece((reordered[0], reordered[1], reordered[2]), "expert", 0, 1, 2)
    w_gate, w_up, w_down = (held_gate, held_up, held_down)
    blocks = devices // EXPERTS
    expert_at = slot_old_at // blocks
    expert_ids = jnp.arange(EXPERTS, dtype=jnp.int32)
    route_hits = route_ids[:, :, None] == expert_ids[None, None, :]
    routed = jnp.any(route_hits, axis=1).astype(jnp.int32)
    position = jnp.cumsum(routed, axis=0) - 1
    bucket_ids = jnp.arange(CAP, dtype=jnp.int32)
    bucket_table = (routed[:, :, None] == 1) & (position[:, :, None] == bucket_ids[None, None, :])
    picker = bucket_table.reshape(tok_rows, EXPERTS * CAP).astype(jnp.bfloat16)
    buckets = lax.dot_general(
        picker, tokens, (((0,), (0,)), ((), ())), preferred_element_type=jnp.float32
    )
    buckets = buckets.astype(jnp.bfloat16).reshape(EXPERTS, CAP, width)
    outgoing = jnp.take(buckets, expert_at, axis=0)
    incoming = lax.all_to_all(outgoing, "expert", split_axis=0, concat_axis=0, tiled=True)
    sources = incoming.shape[0]
    count = incoming.shape[1]
    stacked = incoming.reshape(sources * count, width)
    gate_value = jnp.dot(stacked, w_gate[0], preferred_element_type=jnp.float32)
    up_value = jnp.dot(stacked, w_up[0], preferred_element_type=jnp.float32)
    hidden = (jax.nn.silu(gate_value) * up_value).astype(jnp.bfloat16)
    partial_value = lax.dot_general(
        hidden, w_down[0], (((1,), (1,)), ((), ())), preferred_element_type=jnp.float32
    )
    partial_value = partial_value.astype(jnp.bfloat16).reshape(sources, count, width)
    returned = lax.all_to_all(partial_value, "expert", split_axis=0, concat_axis=0, tiled=True)
    membership = (expert_at[None, :] == expert_ids[:, None]).astype(jnp.bfloat16)
    expert_sum = jnp.dot(
        membership, returned.reshape(devices, CAP * width), preferred_element_type=jnp.float32
    )
    expert_sum = expert_sum.reshape(EXPERTS * CAP, width)
    token_slot = jnp.take_along_axis(position, route_ids, axis=1)
    row_index = route_ids * CAP + token_slot
    selected = jnp.take(expert_sum, row_index.reshape(-1), axis=0).reshape(tok_rows, 2, width)
    first_weight = 1.0 / (1.0 + jnp.exp(route_logits[:, 1] - route_logits[:, 0]))
    second_weight = 1.0 / (1.0 + jnp.exp(route_logits[:, 0] - route_logits[:, 1]))
    weights = jnp.stack([first_weight, second_weight], axis=1)
    combined = jnp.sum(weights[:, :, None] * selected, axis=1).astype(jnp.bfloat16)
    return (combined, migrated[0], migrated[1], migrated[2])


def solution(mesh):
    placed = (
        P(("groups", "expert"), None),
        P(("groups", "expert"), None),
        P(("groups", "expert"), None),
        P(),
        P(),
        P(("groups", "expert"), None, None),
        P(("groups", "expert"), None, None),
        P(("groups", "expert"), None, None),
    )
    return jax.shard_map(
        per_device,
        mesh=mesh,
        in_specs=placed,
        out_specs=(
            P(("groups", "expert"), None),
            P(("groups", "expert"), None, None),
            P(("groups", "expert"), None, None),
            P(("groups", "expert"), None, None),
        ),
        check_vma=False,
    )
```

profile of v0, /device:TPU:46, one launch (start us, length us, event | category | flops | bytes accessed | tf_op | source)
XLA Modules:
  0.0 2042.5 jit_solution(15707181968553112017)
XLA Ops:
  0.6 0.8 select_reduce_fusion.1
  3.1 3.6 gather_fusion
  6.7 6.3 broadcast_select_fusion
  12.9 35.1 %all-to-all-start = ((bf16[64,6,6144]{2,1,0:T(8,128)(2,1)}), bf16[64,6,6144]{2,1,0:T(8,128)(2,1)}, u32[]{:S(2)}, u32[]{:S(2)}) async-start(bf16[64,6,6144]{2,1,0:T(8,128)(2,1)} %broadcast_select_fusion), calls=%async_computation | async-start | bytes 12582912 | tf_op jit(solution)/shard_map/all_to_all | solution.py:61
  48.0 2.0 pad_maximum_fusion
  50.1 88.7 %copy.106 = bf16[1,6144,384]{2,0,1:T(2,128)(2,1)} copy(bf16[1,6144,384]{2,1,0:T(8,128)(2,1)S(1)} %pad_maximum_fusion) | data formatting | bytes 9437184 | tf_op jit(solution)/shard_map/concatenate | solution.py:11
  139.2 101.9 %reduce = bf16[6144,384]{1,0:T(8,128)(2,1)} reduce(bf16[6144,1,384]{2,1,0:T(2,128)(2,1)} %bitcast.53, bf16[]{:T(256)} %broadcast.270), dimensions={1}, to_apply=%bitcast.52.reduce_sub_computation | reduce | bytes 9437186
  241.1 10.5 reshape.275
  251.6 355.0 %all-to-all-done = bf16[64,6,6144]{2,1,0:T(8,128)(2,1)} async-done(((bf16[64,6,6144]{2,1,0:T(8,128)(2,1)}), bf16[64,6,6144]{2,1,0:T(8,128)(2,1)}, u32[]{:S(2)}, u32[]{:S(2)}) %all-to-all-start) | async-done | bytes 4718624 | tf_op jit(solution)/shard_map/all_to_all | solution.py:61
  606.6 7.3 all-to-all-start.2
  614.0 7.8 reshape.202
  621.8 4.2 fusion.3
  626.0 9.5 convolution_convert_fusion
  635.6 7.8 reshape.203
  643.3 394.6 %all-to-all-done.2 = bf16[64,2,18432]{2,1,0:T(2,128)(2,1)} async-done(((bf16[64,2,18432]{2,1,0:T(2,128)(2,1)}), bf16[64,2,18432]{2,1,0:T(2,128)(2,1)}, u32[]{:S(2)}, u32[]{:S(2)}) %all-to-all-start.2) | async-done | bytes 4718624 | tf_op jit(solution)/shard_map/all_to_all | solution.py:13
  1037.9 7.6 all-to-all-start.1
  1045.6 0.8 gather_fusion.2
  1046.4 20.2 reshape.276
  1066.7 4.5 copy.103
  1071.2 2.5 fusion.32
  1073.7 0.8 gather_fusion.4
  1074.5 2.3 gather_fusion.5
  1076.8 3.3 gather_fusion.6
  1080.1 2.1 broadcast_select_fusion.3
  1082.2 2.5 pad_maximum_fusion.1
  1084.6 519.6 %all-to-all-done.1 = bf16[64,6,6144]{2,1,0:T(8,128)(2,1)} async-done(((bf16[64,6,6144]{2,1,0:T(8,128)(2,1)}), bf16[64,6,6144]{2,1,0:T(8,128)(2,1)}, u32[]{:S(2)}, u32[]{:S(2)}) %all-to-all-start.1) | async-done | bytes 4718624 | tf_op jit(solution)/shard_map/all_to_all | solution.py:72
  1604.2 7.6 all-to-all-start.3
  1613.3 5.5 copy.104
  1619.8 0.8 gather_fusion.1
  1621.1 414.6 %all-to-all-done.3 = bf16[64,96,384]{2,1,0:T(8,128)(2,1)} async-done(((bf16[64,96,384]{2,1,0:T(8,128)(2,1)}), bf16[64,96,384]{2,1,0:T(8,128)(2,1)}, u32[]{:S(2)}, u32[]{:S(2)}) %all-to-all-start.3) | async-done | bytes 4718624 | tf_op jit(solution)/shard_map/all_to_all | solution.py:13
  2035.7 4.7 fusion.31
  2040.4 1.9 multiply_reduce_fusion
  (57 shorter events, 5.2 us)
Async XLA Ops:
  0.6 1.9 copy-start
  12.9 35.1 %copy-start.3 = (bf16[1,6144,128]{2,1,0:T(8,128)(2,1)S(1)}, bf16[1,6144,128]{2,1,0:T(8,128)(2,1)}, u32[]{:S(2)}) copy-start(bf16[1,6144,128]{2,1,0:T(8,128)(2,1)} %param.17) | copy-start | bytes 4718596
  12.9 35.1 %copy-start.4 = (bf16[1,6144,128]{2,1,0:T(8,128)(2,1)S(1)}, bf16[1,6144,128]{2,1,0:T(8,128)(2,1)}, u32[]{:S(2)}) copy-start(bf16[1,6144,128]{2,1,0:T(8,128)(2,1)} %param.16) | copy-start | bytes 4718596
  12.9 593.7 %all-to-all-start = ((bf16[64,6,6144]{2,1,0:T(8,128)(2,1)}), bf16[64,6,6144]{2,1,0:T(8,128)(2,1)}, u32[]{:S(2)}, u32[]{:S(2)}) async-start(bf16[64,6,6144]{2,1,0:T(8,128)(2,1)} %broadcast_select_fusion), calls=%async_computation | async-start | bytes 12582912 | tf_op jit(solution)/shard_map/all_to_all | solution.py:61
  606.6 431.2 %all-to-all-start.2 = ((bf16[64,2,18432]{2,1,0:T(2,128)(2,1)}), bf16[64,2,18432]{2,1,0:T(2,128)(2,1)}, u32[]{:S(2)}, u32[]{:S(2)}) async-start(bf16[64,2,18432]{2,1,0:T(2,128)(2,1)} %reshape.275), calls=%async_computation.2 | async-start | bytes 9437184 | tf_op jit(solution)/shard_map/all_to_all | solution.py:13
  643.3 402.2 %copy-start.7 = (s32[64]{0:T(128)S(1)}, s32[64]{0:T(128)}, u32[]{:S(2)}) copy-start(s32[64]{0:T(128)} %param.14) | copy-start | bytes 772
  643.3 402.3 %copy-start.2 = (s32[64]{0:T(128)S(1)}, s32[64]{0:T(128)}, u32[]{:S(2)}) copy-start(s32[64]{0:T(128)} %param.13) | copy-start | bytes 772
  1037.9 566.3 %all-to-all-start.1 = ((bf16[64,6,6144]{2,1,0:T(8,128)(2,1)}), bf16[64,6,6144]{2,1,0:T(8,128)(2,1)}, u32[]{:S(2)}, u32[]{:S(2)}) async-start(bf16[64,6,6144]{2,1,0:T(8,128)(2,1)} %reshape.203), calls=%async_computation.1 | async-start | bytes 12582912 | tf_op jit(solution)/shard_map/all_to_all | solution.py:72
  1084.6 527.2 %copy-start.5 = (s32[16,2]{0,1:T(2,128)S(1)}, s32[16,2]{0,1:T(2,128)}, u32[]{:S(2)}) copy-start(s32[16,2]{0,1:T(2,128)} %param.11) | copy-start | bytes 388
  1604.2 431.5 %all-to-all-start.3 = ((bf16[64,96,384]{2,1,0:T(8,128)(2,1)}), bf16[64,96,384]{2,1,0:T(8,128)(2,1)}, u32[]{:S(2)}, u32[]{:S(2)}) async-start(bf16[64,96,384]{2,1,0:T(8,128)(2,1)} %pad_maximum_fusion.1), calls=%async_computation.3 | async-start | bytes 9437184 | tf_op jit(solution)/shard_map/all_to_all | solution.py:13
  1612.0 1.2 copy-start.6
  2035.7 6.5 copy-start.1
where the time goes:
time: 2050 us; the launch traced here: 2040 us
  waiting for transfers between devices  1680 us (82%)
  local copies, waits for them, and re-layouts  167 us (8%)
  other arithmetic  118 us (6%)
  starting transfers between devices  57.6 us (3%)
    all_to_all x2, waiting for transfers between devices, in_one_piece(): lax.all_to_all(both, axis, split_axis=split_dim, concat_axis=concat_dim,...  809 us
    all_to_all x1, waiting for transfers between devices, per_device(): lax.all_to_all(partial_value, 'expert', split_axis=0, concat_axis=0, tile...  520 us
    all_to_all x1, waiting for transfers between devices, per_device(): lax.all_to_all(outgoing, 'expert', split_axis=0, concat_axis=0, tiled=True)  355 us
    unnamed x1, other arithmetic  102 us
    concatenate x1, local copies, waits for them, and re-layouts, in_one_piece(): both = jnp.concatenate(arrays, axis=along)  88.7 us
    unnamed x21, local copies, waits for them, and re-layouts  41.2 us
  transfers between devices with their start and end apart: 4, of which 4 were waited for; matrix products, arithmetic and copies ran while one was open for 14% of the time, Pallas kernels for 0%

commit v1 on v0

v1 whole, which is shorter than its diff:
```python
import jax
import jax.numpy as jnp
from jax import lax
from jax.sharding import PartitionSpec as P

EXPERTS = 8
EXTRA = 128


def inverse_of(placement, device_ids):
    return jnp.sum(
        jnp.where(placement[:, None] == device_ids[None, :], device_ids[:, None], 0), axis=0
    )


def exact_parts(v):
    first = lax.reduce_precision(v, 8, 7)
    rest = v - first
    second = lax.reduce_precision(rest, 8, 7)
    return first, second, rest - second


def per_device(
    tokens, route_ids, route_logits, old_place, new_place, held_gate, held_up, held_down
):
    devices = lax.axis_size("expert")
    rows, width = tokens.shape
    device_ids = jnp.arange(devices, dtype=jnp.int32)
    slot_new_at = inverse_of(new_place, device_ids)
    slot_old_at = inverse_of(old_place, device_ids)
    source_of = jnp.take(old_place, slot_new_at)

    moved = []
    for held in (held_gate, held_up, held_down):
        f = held.shape[2]
        bands = held.reshape(devices, held.shape[1] // devices, f)
        spread = lax.all_to_all(bands, "expert", split_axis=0, concat_axis=0, tiled=True)
        ordered = jnp.take(spread, source_of, axis=0)
        back = lax.all_to_all(ordered, "expert", split_axis=0, concat_axis=0, tiled=True)
        moved.append(back.reshape(held.shape))

    w0 = 1.0 / (1.0 + jnp.exp(route_logits[:, 1] - route_logits[:, 0]))
    w1 = 1.0 / (1.0 + jnp.exp(route_logits[:, 0] - route_logits[:, 1]))
    columns = [route_ids[:, 0].astype(jnp.float32), route_ids[:, 1].astype(jnp.float32)]
    columns += list(exact_parts(w0)) + list(exact_parts(w1))
    side = jnp.stack(columns, axis=1).astype(jnp.bfloat16)
    side = jnp.pad(side, ((0, 0), (0, EXTRA - side.shape[1])))
    packed = jnp.concatenate([tokens, side], axis=1)
    gathered = lax.all_gather(packed, "expert", axis=0, tiled=True)
    everyone = gathered[:, :width]
    info = gathered[:, width : width + 8].astype(jnp.float32)

    blocks = devices // EXPERTS
    me = lax.axis_index("expert")
    expert = (jnp.take(slot_old_at, me) // blocks).astype(jnp.float32)
    g0 = info[:, 2] + info[:, 3] + info[:, 4]
    g1 = info[:, 5] + info[:, 6] + info[:, 7]
    share = jnp.where(info[:, 0] == expert, g0, 0.0) + jnp.where(info[:, 1] == expert, g1, 0.0)
    gate_value = jnp.dot(everyone, held_gate[0], preferred_element_type=jnp.float32)
    up_value = jnp.dot(everyone, held_up[0], preferred_element_type=jnp.float32)
    hidden = (jax.nn.silu(gate_value) * up_value).astype(jnp.bfloat16)
    partial = lax.dot_general(
        hidden, held_down[0], (((1,), (1,)), ((), ())), preferred_element_type=jnp.float32
    )
    term = (share[:, None] * partial).astype(jnp.bfloat16)
    combined = lax.psum_scatter(term, "expert", scatter_dimension=0, tiled=True)
    return (combined, *moved)


def solution(mesh):
    split = P(("groups", "expert"))
    return jax.shard_map(
        per_device,
        mesh=mesh,
        in_specs=(split, split, split, P(), P(), split, split, split),
        out_specs=(split, split, split, split),
        check_vma=False,
    )
```

time: 2050 us -> 1140 us (0.56)
  waiting for transfers between devices: 1680 us -> 682 us
  blocking collectives: 0 us -> 358 us
  local copies, waits for them, and re-layouts: 167 us -> 14.6 us
  other arithmetic: 118 us -> 7.16 us
  starting transfers between devices: 57.6 us -> 27.8 us
    all_to_all x4, waiting for transfers between devices: 1680 us -> 575 us  [the longest x2 331 us: per_device(): lax.all_to_all(bands, 'expert', split_axis=0, concat_axis=0, tiled=True)]
    all_to_all x0 -> x2, blocking collectives: none -> 358 us  [the longest x1 188 us: per_device(): lax.all_to_all(bands, 'expert', split_axis=0, concat_axis=0, tiled=True)]
    unnamed x1 -> x0, other arithmetic: 102 us -> none
    concatenate x1 -> x0, local copies, waits for them, and re-layouts: 88.7 us -> none  [in_one_piece(): both = jnp.concatenate(arrays, axis=along)]
    reduce_scatter x0 -> x1, waiting for transfers between devices: none -> 62.8 us  [per_device(): combined = lax.psum_scatter(term, 'expert', scatter_dimension=0, tiled=True)]
    all_gather x0 -> x1, waiting for transfers between devices: none -> 43.5 us  [per_device(): gathered = lax.all_gather(packed, 'expert', axis=0, tiled=True)]
    unnamed x21 -> x22, local copies, waits for them, and re-layouts: 41.2 us -> 5.73 us
    all_to_all x4, starting transfers between devices: 57.6 us -> 27.4 us  [the longest x2 14.4 us: per_device(): lax.all_to_all(bands, 'expert', split_axis=0, concat_axis=0, tiled=True)]
  transfers between devices with their start and end apart: 4 -> 6, of which waited for: 4 -> 6; matrix products, arithmetic and copies ran while one was open for 14% -> 4% of each run, Pallas kernels for 0% -> 0%
where the time goes in v1:
time: 1140 us; the launch traced here: 1130 us
  waiting for transfers between devices  682 us (60%)
  blocking collectives  358 us (31%)
  starting transfers between devices  27.8 us (2%)
  matrix products  26.9 us (2%)
  between operations  14.8 us (1%)
  local copies, waits for them, and re-layouts  14.6 us (1%)
    all_to_all x2, waiting for transfers between devices, per_device(): lax.all_to_all(bands, 'expert', split_axis=0, concat_axis=0, tiled=True)  331 us
    all_to_all x2, waiting for transfers between devices, per_device(): lax.all_to_all(ordered, 'expert', split_axis=0, concat_axis=0, tiled=True)  244 us
    all_to_all x1, blocking collectives, per_device(): lax.all_to_all(bands, 'expert', split_axis=0, concat_axis=0, tiled=True)  188 us
    all_to_all x1, blocking collectives, per_device(): lax.all_to_all(ordered, 'expert', split_axis=0, concat_axis=0, tiled=True)  170 us
    reduce_scatter x1, waiting for transfers between devices, per_device(): combined = lax.psum_scatter(term, 'expert', scatter_dimension=0, tiled=True)  62.8 us
    all_gather x1, waiting for transfers between devices, per_device(): gathered = lax.all_gather(packed, 'expert', axis=0, tiled=True)  43.5 us
  transfers between devices with their start and end apart: 6, of which 6 were waited for; matrix products, arithmetic and copies ran while one was open for 4% of the time, Pallas kernels for 0%

profile of v1, /device:TPU:46, one launch (start us, length us, event | category | flops | bytes accessed | tf_op | source)
XLA Modules:
  0.0 1131.0 jit_solution(2998658887362581671)
XLA Ops:
  7.2 188.4 %all_to_all.30 = bf16[64,96,128]{2,1,0:T(8,128)(2,1)} all-to-all(bf16[64,96,128]{2,1,0:T(8,128)(2,1)} %bitcast.30), channel_id=1, replica_groups=mesh['groups'=4,'expert'=64] {'expert'}, dimensions={0} | all-to-all | bytes 3145728 | tf_op jit(solution)/shard_map/all_to_all | solution.py:37
  195.6 6.9 all-to-all-start.2
  202.8 0.7 fusion.32
  203.5 165.7 %all-to-all-done.2 = bf16[64,96,128]{2,1,0:T(8,128)(2,1)S(1)} async-done(((bf16[64,96,128]{2,1,0:T(8,128)(2,1)}), bf16[64,96,128]{2,1,0:T(8,128)(2,1)S(1)}, u32[]{:S(2)}, u32[]{:S(2)}) %all-to-all-start.2) | async-done | bytes 1572896 | tf_op jit(solution)/shard_map/all_to_all | solution.py:37
  369.2 7.5 all-to-all-start.4
  376.7 0.1 select_reduce_fusion
  376.9 0.8 gather_fusion
  377.7 2.3 gather_fusion.1
  379.9 1.9 gather_fusion.2
  381.8 165.7 %all-to-all-done.4 = bf16[64,96,128]{2,1,0:T(8,128)(2,1)} async-done(((bf16[64,96,128]{2,1,0:T(8,128)(2,1)}), bf16[64,96,128]{2,1,0:T(8,128)(2,1)}, u32[]{:S(2)}, u32[]{:S(2)}) %all-to-all-start.4) | async-done | bytes 1572896 | tf_op jit(solution)/shard_map/all_to_all | solution.py:37
  547.5 3.3 gather_fusion.3
  550.9 4.1 broadcast_select_fusion
  554.9 6.5 all-to-all-start.1
  561.5 0.2 reduce-scatter.2.cloned.1.call-start
  561.7 0.1 select_reduce_fusion.1
  561.8 0.6 dynamic-slice.2
  563.0 43.5 %all-gather.2.cloned.1.call-done = bf16[1024,6272]{1,0:T(8,128)(2,1)} async-done(((bf16[16,6272]{1,0:T(8,128)(2,1)}), bf16[1024,6272]{1,0:T(8,128)(2,1)}) %all-gather.2.cloned.1.call-update) | async-done | bytes 12845072 | tf_op jit(solution)/shard_map/all_gather | solution.py:49
  606.5 1.0 slice_convert_fusion
  607.5 1.2 fusion.23
  608.6 0.2 copy-done.4
  608.9 7.2 fusion.2
  616.1 19.7 %multiply_convert_fusion = bf16[1024,6144]{1,0:T(8,128)(2,1)} fusion(f32[1024]{0:T(1024)S(1)} %fusion.23, bf16[1,6144,128]{2,1,0:T(8,128)(2,1)} %param.17, bf16[1,6144,128]{2,1,0:T(8,128)(2,1)} %param.16, bf16[1024,6272]{1,0:T(8,128)(2,1)} %all-gather.2.cloned.1.call-done, f32[1024,128]{1,0:T(8,128)} %fusion.2), kind=kOutput, calls=%fused_computation.4 | convolution fusion | flops 3234594816 | bytes 28839936 | tf_op jit(solution)/shard_map/dot_general | solution.py:62
  635.8 81.2 %all-to-all-done.1 = bf16[64,96,128]{2,1,0:T(8,128)(2,1)S(1)} async-done(((bf16[64,96,128]{2,1,0:T(8,128)(2,1)}), bf16[64,96,128]{2,1,0:T(8,128)(2,1)S(1)}, u32[]{:S(2)}, u32[]{:S(2)}) %all-to-all-start.1) | async-done | bytes 1572896 | tf_op jit(solution)/shard_map/all_to_all | solution.py:39
  717.0 169.8 %all_to_all.31 = bf16[64,96,128]{2,1,0:T(8,128)(2,1)} all-to-all(bf16[64,96,128]{2,1,0:T(8,128)(2,1)S(1)} %get-tuple-element.27), channel_id=1, replica_groups=mesh['groups'=4,'expert'=64] {'expert'}, dimensions={0} | all-to-all | bytes 3145728 | tf_op jit(solution)/shard_map/all_to_all | solution.py:39
  886.8 6.5 all-to-all-start.5
  893.3 162.6 %all-to-all-done.5 = bf16[64,96,128]{2,1,0:T(8,128)(2,1)S(1)} async-done(((bf16[64,96,128]{2,1,0:T(8,128)(2,1)}), bf16[64,96,128]{2,1,0:T(8,128)(2,1)S(1)}, u32[]{:S(2)}, u32[]{:S(2)}) %all-to-all-start.5) | async-done | bytes 1572896 | tf_op jit(solution)/shard_map/all_to_all | solution.py:39
  1055.9 1.1 copy-done.2
  1057.1 62.8 %reduce-scatter.2.cloned.1.call-done = bf16[16,6144]{1,0:T(8,128)(2,1)} async-done(((bf16[1024,6144]{1,0:T(8,128)(2,1)}), bf16[16,6144]{1,0:T(8,128)(2,1)}) %reduce-scatter.2.cloned.1.call-update) | async-done | bytes 196624 | tf_op jit(solution)/shard_map/reduce_scatter | solution.py:66
  1119.9 1.1 copy.19
  1121.0 1.1 copy.20
  1122.2 0.8 copy-done.3
  1123.0 1.1 copy.21
  (27 shorter events, 0.4 us)
Async XLA Ops:
  195.6 7.0 copy-start.7
  195.6 7.0 copy-start.6
  195.6 7.1 copy-start.5
  195.6 173.6 %all-to-all-start.2 = ((bf16[64,96,128]{2,1,0:T(8,128)(2,1)}), bf16[64,96,128]{2,1,0:T(8,128)(2,1)S(1)}, u32[]{:S(2)}, u32[]{:S(2)}) async-start(bf16[64,96,128]{2,1,0:T(8,128)(2,1)} %bitcast.9), calls=%async_computation.3 | async-start | bytes 3145728 | tf_op jit(solution)/shard_map/all_to_all | solution.py:37
  202.5 404.0 %all-gather.2.cloned.1.call-start = ((), (), s32[]{:S(2)}) async-start(), calls=%async_computation.7 | async-start | bytes 13045760 | tf_op jit(solution)/shard_map/all_gather | solution.py:49
  369.2 7.5 copy-start.8
  369.2 7.6 copy-start
  369.2 178.3 %all-to-all-start.4 = ((bf16[64,96,128]{2,1,0:T(8,128)(2,1)}), bf16[64,96,128]{2,1,0:T(8,128)(2,1)}, u32[]{:S(2)}, u32[]{:S(2)}) async-start(bf16[64,96,128]{2,1,0:T(8,128)(2,1)} %bitcast.11), calls=%async_computation.5 | async-start | bytes 3145728 | tf_op jit(solution)/shard_map/all_to_all | solution.py:37
  554.9 162.1 %all-to-all-start.1 = ((bf16[64,96,128]{2,1,0:T(8,128)(2,1)}), bf16[64,96,128]{2,1,0:T(8,128)(2,1)S(1)}, u32[]{:S(2)}, u32[]{:S(2)}) async-start(bf16[64,96,128]{2,1,0:T(8,128)(2,1)} %get-tuple-element.28), calls=%async_computation.2 | async-start | bytes 3145728 | tf_op jit(solution)/shard_map/all_to_all | solution.py:39
  561.5 558.4 %reduce-scatter.2.cloned.1.call-start = ((), (), s32[]{:S(2)}) async-start(), calls=%async_computation.8 | async-start | bytes 12779520 | tf_op jit(solution)/shard_map/reduce_scatter | solution.py:66
  607.5 1.4 copy-start.4
  886.8 169.2 %all-to-all-start.5 = ((bf16[64,96,128]{2,1,0:T(8,128)(2,1)}), bf16[64,96,128]{2,1,0:T(8,128)(2,1)S(1)}, u32[]{:S(2)}, u32[]{:S(2)}) async-start(bf16[64,96,128]{2,1,0:T(8,128)(2,1)} %get-tuple-element.26), calls=%async_computation.6 | async-start | bytes 3145728 | tf_op jit(solution)/shard_map/all_to_all | solution.py:39
  1055.9 1.1 copy-start.2
  1057.1 63.9 %copy-start.1 = (bf16[64,96,128]{2,1,0:T(8,128)(2,1)S(1)}, bf16[64,96,128]{2,1,0:T(8,128)(2,1)}, u32[]{:S(2)}) copy-start(bf16[64,96,128]{2,1,0:T(8,128)(2,1)} %all_to_all.31) | copy-start | bytes 4718596
  1121.0 2.0 copy-start.3
Sparse Core Ops, SparseCore 0:
  205.8 400.6 all-gather.1
  635.9 483.8 reduce-scatter.1
